TPU v7x, 32 devices: a whole 2x2x4 slice. The times are simulated.
32 devices in a mesh: row: 4 (over y, x), col: 8 (over z, core).
Axes of the slice: x: 2, y: 2, z: 4, core: 2. Of those that a mesh axis runs over, the one named last changes fastest.
Arguments:
- covariance: float32 [16384, 16384], P('row', 'col'), may hold values from -1 to 560
- seed_index: int32 [128], replicated, may hold values from 0 to 16383, as said below
Outputs:
- basis: float32 [16384, 384], P('row')
- projection: float32 [384, 256], replicated
- first_pass: float32 [384, 256], replicated
Inputs may be any that keep to these rules, and one draw needn't show every extreme that they name: `seed_index`: 128 distinct column indices.
All inputs are finite; a program needn't handle non-finite values.
Results may differ from a plain program's by a relative error of at most 0.00019.
Values sent between devices are 32-bit elements; how exact they have to be, the bound alone decides.
A program may use at most 128 MiB of HBM per device.

v0:
```python
import jax
import jax.numpy as jnp
from jax import lax
from jax.sharding import PartitionSpec as P

N = 16384
ITERS = 2


def product(left, right):
    return jnp.dot(left, right, precision=lax.Precision.HIGHEST, preferred_element_type=jnp.float32)


def finish_block(block, gram):
    lower = jnp.linalg.cholesky(gram)
    basis_block = jax.scipy.linalg.solve_triangular(lower, block.T, lower=True).T
    return (basis_block, lower.T)


def transpose_block(current, col_place, col_count):
    whole = lax.all_gather(current, "row", axis=0, tiled=True)
    vector = lax.dynamic_slice_in_dim(whole, col_place * col_count, col_count, 0)
    return vector


def local(covariance, seed_index):
    col_count = covariance.shape[1]
    width = seed_index.shape[0]
    col_place = lax.axis_index("col")
    offsets = seed_index - col_place * col_count
    inside = (offsets >= 0) & (offsets < col_count)
    picked = jnp.take(covariance, jnp.clip(offsets, 0, col_count - 1), axis=1)
    start = lax.psum(jnp.where(inside[None, :], picked, 0.0), "col")
    gram = lax.psum(product(start.T, start), "row")
    current, upper = finish_block(start, gram)
    full = current
    blocks = [current]
    projection = jnp.zeros(((ITERS + 1) * width, ITERS * width), jnp.float32)
    first_pass = jnp.zeros(((ITERS + 1) * width, ITERS * width), jnp.float32)
    for section in range(ITERS):
        vector = transpose_block(full, col_place, col_count)
        partial_value = product(covariance, vector)
        stacked = jnp.concatenate(blocks, axis=1)
        image = lax.psum(partial_value, "col")
        first = lax.psum(product(stacked.T, image), "row")
        once = image - product(stacked, first)
        second, raw_gram = lax.psum((product(stacked.T, once), product(once.T, once)), "row")
        twice = once - product(stacked, second)
        gram = raw_gram - product(second.T, second)
        current, upper = finish_block(twice, gram)
        projection = projection.at[
            : (section + 1) * width, section * width : (section + 1) * width
        ].set(first + second)
        projection = projection.at[
            (section + 1) * width : (section + 2) * width, section * width : (section + 1) * width
        ].set(upper)
        first_pass = first_pass.at[
            : (section + 1) * width, section * width : (section + 1) * width
        ].set(first)
        blocks.append(current)
        full = current
    basis = jnp.concatenate(blocks, axis=1) * jnp.float32(N**0.5)
    return (basis, projection, first_pass)


def solution(mesh):
    return jax.shard_map(
        local,
        mesh=mesh,
        in_specs=(P("row", "col"), P()),
        out_specs=(P("row", None), P(), P()),
        check_vma=False,
    )
```

profile of v0, /device:TPU:0, one launch (start us, length us, event | category | flops | bytes accessed | tf_op | source)
XLA Modules:
  0.0 872.3 jit_solution(4701074359064413226)
XLA Ops:
  7.9 31.2 %copy.5 = f32[4096,2048]{0,1:T(8,128)} copy(f32[4096,2048]{1,0:T(8,128)} %param.17) | data formatting | bytes 67108864 | tf_op args[0]
  39.1 12.8 %gather_fusion = f32[128,4096]{1,0:T(8,128)S(1)} fusion(f32[4096,2048]{0,1:T(8,128)} %copy.5, s32[1024]{0:T(1024)S(1)} %pad_clamp_fusion), kind=kCustom, calls=%fused_computation | custom fusion | bytes 4194816 | tf_op jit(solution)/shard_map/jit(_take)/gather | solution.py:32
  53.6 68.0 %all-reduce.13.cloned.1.call-done = f32[4096,128]{0,1:T(8,128)} async-done(((f32[4096,128]{0,1:T(8,128)}), f32[4096,128]{0,1:T(8,128)}) %all-reduce.13.cloned.1.call-update) | async-done | bytes 2097168 | tf_op jit(solution)/shard_map/psum | solution.py:33
  121.6 4.8 fusion.25
  127.0 41.0 %all-reduce.15.cloned.1.call-done = f32[128,128]{0,1:T(8,128)} async-done(((f32[128,128]{0,1:T(8,128)}), f32[128,128]{0,1:T(8,128)}) %all-reduce.15.cloned.1.call-update) | async-done | bytes 65552 | tf_op jit(solution)/shard_map/psum | solution.py:34
  169.8 11.7 %cholesky.59 = f32[128,128]{1,0:T(8,128)S(1)} custom-call(f32[128,128]{1,0:T(8,128)S(1)} %fusion.15), custom_call_target="Cholesky" | custom-call | tf_op jit(solution)/shard_map/jit(cholesky)/cholesky | solution.py:15
  182.9 9.8 %custom-call.7 = f32[1,128,128]{1,2,0:T(8,128)S(1)} custom-call(f32[1,128,128]{2,1,0:T(8,128)S(1)} %fusion.9), custom_call_target="InvertDiagBlocksLowerTriangular" | custom-call | tf_op jit(solution)/shard_map/jit(_solve_triangular)/triangular_solve | solution.py:16
  192.7 3.2 fusion.2
  196.2 87.4 %all-gather.3.cloned.1.call-done = f32[16384,128]{0,1:T(8,128)} async-done(((f32[4096,128]{0,1:T(8,128)}), f32[16384,128]{0,1:T(8,128)}) %all-gather.3.cloned.1.call-update) | async-done | bytes 8388624 | tf_op jit(solution)/shard_map/all_gather | solution.py:21
  283.6 39.2 %convolution_bitcast_fusion.3 = f32[4096,128]{0,1:T(8,128)} fusion(f32[4096,2048]{1,0:T(8,128)} %param.17, f32[16384,128]{0,1:T(8,128)} %all-gather.3.cloned.1.call-done, s32[]{:T(128)S(6)} %select_n.23), kind=kOutput, calls=%fused_computation.11 | convolution fusion | flops 12884901888 | bytes 36700164 | tf_op jit(solution)/shard_map/dot_general | solution.py:11
  322.9 65.3 %all-reduce.17.cloned.1.call-done = f32[4096,128]{0,1:T(8,128)} async-done(((f32[4096,128]{0,1:T(8,128)}), f32[4096,128]{0,1:T(8,128)}) %all-reduce.17.cloned.1.call-update) | async-done | bytes 2097168 | tf_op jit(solution)/shard_map/psum | solution.py:44
  388.2 4.0 fusion.26
  392.5 41.3 %all-reduce.19.cloned.1.call-done = f32[128,128]{1,0:T(8,128)} async-done(((f32[128,128]{1,0:T(8,128)}), f32[128,128]{1,0:T(8,128)}) %all-reduce.19.cloned.1.call-update) | async-done | bytes 65552 | tf_op jit(solution)/shard_map/psum | solution.py:45
  433.9 3.7 convolution_subtract_fusion.3
  442.8 42.1 %all-reduce.27.cloned.1.call-done = (f32[128,128]{1,0:T(8,128)}, f32[128,128]{0,1:T(8,128)}) async-done(((f32[128,128]{1,0:T(8,128)}, f32[128,128]{0,1:T(8,128)}), (f32[128,128]{1,0:T(8,128)}, f32[128,128]{0,1:T(8,128)})) %all-reduce.27.cloned.1.call-update) | async-done | bytes 131088 | tf_op jit(solution)/shard_map/psum | solution.py:47
  484.9 5.0 fusion.1
  490.3 11.7 %cholesky.70 = f32[128,128]{1,0:T(8,128)S(1)} custom-call(f32[128,128]{1,0:T(8,128)S(1)} %fusion.13), custom_call_target="Cholesky" | custom-call | tf_op jit(solution)/shard_map/jit(cholesky)/cholesky | solution.py:15
  503.4 9.8 %custom-call.8 = f32[1,128,128]{1,2,0:T(8,128)S(1)} custom-call(f32[1,128,128]{2,1,0:T(8,128)S(1)} %get-tuple-element.91), custom_call_target="InvertDiagBlocksLowerTriangular" | custom-call | tf_op jit(solution)/shard_map/jit(_solve_triangular)/triangular_solve | solution.py:16
  513.2 4.9 convolution_bitcast_fusion.2
  518.6 87.1 %all-gather.5.cloned.1.call-done = f32[16384,128]{0,1:T(8,128)} async-done(((f32[4096,128]{0,1:T(8,128)}), f32[16384,128]{0,1:T(8,128)}) %all-gather.5.cloned.1.call-update) | async-done | bytes 8388624 | tf_op jit(solution)/shard_map/all_gather | solution.py:21
  605.7 39.1 %convolution_bitcast_fusion.1 = f32[4096,128]{0,1:T(8,128)} fusion(f32[4096,2048]{1,0:T(8,128)} %param.17, f32[16384,128]{0,1:T(8,128)} %all-gather.5.cloned.1.call-done, s32[]{:T(128)S(6)} %select_n.23), kind=kOutput, calls=%fused_computation.6 | convolution fusion | flops 12884901888 | bytes 36700164 | tf_op jit(solution)/shard_map/dot_general | solution.py:11
  644.9 65.2 %all-reduce.21.cloned.1.call-done = f32[4096,128]{0,1:T(8,128)} async-done(((f32[4096,128]{0,1:T(8,128)}), f32[4096,128]{0,1:T(8,128)}) %all-reduce.21.cloned.1.call-update) | async-done | bytes 2097168 | tf_op jit(solution)/shard_map/psum | solution.py:44
  710.2 6.3 fusion.5
  717.4 41.1 %all-reduce.23.cloned.1.call-done = f32[256,128]{1,0:T(8,128)} async-done(((f32[256,128]{1,0:T(8,128)}), f32[256,128]{1,0:T(8,128)}) %all-reduce.23.cloned.1.call-update) | async-done | bytes 131088 | tf_op jit(solution)/shard_map/psum | solution.py:45
  758.5 5.0 convolution_subtract_fusion.1
  763.5 4.1 fusion.4
  770.8 42.0 %all-reduce.25.cloned.1.call-done = (f32[256,128]{1,0:T(8,128)}, f32[128,128]{0,1:T(8,128)}) async-done(((f32[256,128]{1,0:T(8,128)}, f32[128,128]{0,1:T(8,128)}), (f32[256,128]{1,0:T(8,128)}, f32[128,128]{0,1:T(8,128)})) %all-reduce.25.cloned.1.call-update) | async-done | bytes 196624 | tf_op jit(solution)/shard_map/psum | solution.py:47
  812.8 6.1 fusion
  824.6 11.7 %cholesky.81 = f32[128,128]{1,0:T(8,128)S(1)} custom-call(f32[128,128]{1,0:T(8,128)S(1)} %fusion.11), custom_call_target="Cholesky" | custom-call | tf_op jit(solution)/shard_map/jit(cholesky)/cholesky | solution.py:15
  837.7 9.8 %custom-call.9 = f32[1,128,128]{1,2,0:T(8,128)S(1)} custom-call(f32[1,128,128]{2,1,0:T(8,128)S(1)} %get-tuple-element.89), custom_call_target="InvertDiagBlocksLowerTriangular" | custom-call | tf_op jit(solution)/shard_map/jit(_solve_triangular)/triangular_solve | solution.py:16
  847.6 3.6 convolution_bitcast_fusion
  854.3 6.6 copy.18
  (85 shorter events, 32.7 us)
Async XLA Ops:
  7.2 114.4 %all-reduce.13.cloned.1.call-start = ((), (), s32[]{:S(2)}) async-start(), calls=%async_computation | async-start | bytes 4194304 | tf_op jit(solution)/shard_map/psum | solution.py:33
  53.5 114.5 %all-reduce.15.cloned.1.call-start = ((), (), s32[]{:S(2)}) async-start(), calls=%async_computation.1 | async-start | bytes 131072 | tf_op jit(solution)/shard_map/psum | solution.py:34
  121.6 71.1 %copy-start.5 = (f32[4096,128]{0,1:T(8,128)S(1)}, f32[4096,128]{0,1:T(8,128)}, u32[]{:S(2)}) copy-start(f32[4096,128]{0,1:T(8,128)} %all-reduce.13.cloned.1.call-done) | copy-start | bytes 6291460
  126.4 157.2 %all-gather.3.cloned.1.call-start = ((), (), s32[]{:S(2)}) async-start(), calls=%async_computation.2 | async-start | bytes 10485760 | tf_op jit(solution)/shard_map/all_gather | solution.py:21
  196.0 192.2 %all-reduce.17.cloned.1.call-start = ((), (), s32[]{:S(2)}) async-start(), calls=%async_computation.3 | async-start | bytes 4194304 | tf_op jit(solution)/shard_map/psum | solution.py:44
  322.8 65.3 %copy-start = (f32[128,4096]{1,0:T(8,128)S(1)}, f32[128,4096]{1,0:T(8,128)}, u32[]{:S(2)}) copy-start(f32[128,4096]{1,0:T(8,128)} %fusion.2) | copy-start | bytes 6291460
  322.9 111.0 %all-reduce.19.cloned.1.call-start = ((), (), s32[]{:S(2)}) async-start(), calls=%async_computation.4 | async-start | bytes 131072 | tf_op jit(solution)/shard_map/psum | solution.py:45
  392.2 92.7 %all-reduce.27.cloned.1.call-start = ((), (), s32[]{:S(2)}) async-start(), calls=%async_computation.9 | async-start | bytes 262144 | tf_op jit(solution)/shard_map/psum | solution.py:47
  437.6 2.5 copy-start.3
  442.5 163.2 %all-gather.5.cloned.1.call-start = ((), (), s32[]{:S(2)}) async-start(), calls=%async_computation.5 | async-start | bytes 10485760 | tf_op jit(solution)/shard_map/all_gather | solution.py:21
  484.9 5.0 copy-start.8
  484.9 5.0 copy-start.13
  518.1 192.1 %all-reduce.21.cloned.1.call-start = ((), (), s32[]{:S(2)}) async-start(), calls=%async_computation.6 | async-start | bytes 4194304 | tf_op jit(solution)/shard_map/psum | solution.py:44
  644.9 113.6 %all-reduce.23.cloned.1.call-start = ((), (), s32[]{:S(2)}) async-start(), calls=%async_computation.7 | async-start | bytes 262144 | tf_op jit(solution)/shard_map/psum | solution.py:45
  716.5 96.3 %all-reduce.25.cloned.1.call-start = ((), (), s32[]{:S(2)}) async-start(), calls=%async_computation.8 | async-start | bytes 393216 | tf_op jit(solution)/shard_map/psum | solution.py:47
  758.5 5.0 copy-start.1
  763.5 4.1 copy-start.4
  767.6 3.1 copy-start.7
  812.8 6.1 copy-start.6
  812.8 6.1 copy-start.10
  812.8 11.2 %copy-start.12 = (f32[128,128]{0,1:T(8,128)S(1)}, f32[128,128]{0,1:T(8,128)}, u32[]{:S(2)}) copy-start(f32[128,128]{0,1:T(8,128)} %get-tuple-element.81) | copy-start | bytes 196612
  847.5 3.7 copy-start.2
  863.7 0.7 copy-start.11
  864.4 0.7 copy-start.9
Sparse Core Ops, SparseCore 0:
  53.6 67.8 all-reduce.12
  126.5 41.4 all-reduce.14
  196.1 87.4 all-gather.2
  323.0 65.1 all-reduce.16
  392.4 41.4 all-reduce.18
  442.6 42.2 all-reduce.26
  518.2 87.4 all-gather.4
  645.0 65.1 all-reduce.20
  716.6 41.8 all-reduce.22
  770.1 42.6 all-reduce.24
where the time goes:
time: 877 us; the launch traced here: 872 us
  waiting for transfers between devices  581 us (66%)
  matrix products  137 us (16%)
  other arithmetic  77.5 us (9%)
  local copies, waits for them, and re-layouts  59.9 us (7%)
  between operations  14.7 us (2%)
    all_gather x2, waiting for transfers between devices, transpose_block(): whole = lax.all_gather(current, 'row', axis=0, tiled=True)  175 us
    psum x2, waiting for transfers between devices, local(): image = lax.psum(partial_value, 'col')  130 us
    dot_general x15, matrix products, product(): jnp.dot(left, right, precision=lax.Precision.HIGHEST, preferred_element_t...  125 us
    psum x2, waiting for transfers between devices, local(): lax.psum((product(stacked.T, once), product(once.T, once)), 'row')  84.1 us
    psum x2, waiting for transfers between devices, local(): first = lax.psum(product(stacked.T, image), 'row')  82.4 us
    psum x1, waiting for transfers between devices, local(): start = lax.psum(jnp.where(inside[None, :], picked, 0.0), 'col')  68 us
    psum x1, waiting for transfers between devices, local(): gram = lax.psum(product(start.T, start), 'row')  41 us
    unnamed x30, local copies, waits for them, and re-layouts  39.2 us
  transfers between devices with their start and end apart: 10, of which 10 were waited for; matrix products, arithmetic and copies ran while one was open for 0% of the time, Pallas kernels for 0%

commit v1 on v0

v1 whole, which is shorter than its diff:
```python
import jax
import jax.numpy as jnp
from jax import lax
from jax.sharding import PartitionSpec as P

N = 16384
ITERS = 2


def product(left, right):
    return jnp.dot(left, right, precision=lax.Precision.HIGH, preferred_element_type=jnp.float32)


def small_sum(value, axis):
    return jnp.sum(lax.all_gather(value, axis, axis=0), axis=0)


def finish_block(block, gram):
    lower = jnp.linalg.cholesky(gram)
    basis_block = jax.scipy.linalg.solve_triangular(lower, block.T, lower=True).T
    return (basis_block, lower.T)


def to_row_layout(piece, rows, cols):
    perm = [(r * cols + c, c * rows + r) for r in range(rows) for c in range(cols)]
    moved = lax.ppermute(piece, ("row", "col"), perm)
    return lax.all_gather(moved, "col", axis=0, tiled=True)


def solve(rows, cols, covariance, seed_index):
    row_count, col_count = covariance.shape
    width = seed_index.shape[0]
    row_place = lax.axis_index("row")
    piece_count = col_count // rows
    offsets = seed_index - row_place * row_count
    inside = (offsets >= 0) & (offsets < row_count)
    picked = jnp.take(covariance, jnp.clip(offsets, 0, row_count - 1), axis=0)
    start = lax.psum(jnp.where(inside[:, None], picked, 0.0), "row").T
    gram = small_sum(product(start.T, start), "col")
    vector, upper = finish_block(start, gram)
    piece = lax.dynamic_slice_in_dim(vector, row_place * piece_count, piece_count, 0)
    current = to_row_layout(piece, rows, cols)
    blocks = [current]
    projection = jnp.zeros(((ITERS + 1) * width, ITERS * width), jnp.float32)
    first_pass = jnp.zeros(((ITERS + 1) * width, ITERS * width), jnp.float32)
    for section in range(ITERS):
        stacked = jnp.concatenate(blocks, axis=1)
        if section == 0:
            image = lax.psum(product(covariance, vector), "col")
        else:
            partial_value = product(current.T, covariance).T
            piece = lax.psum_scatter(partial_value, "row", scatter_dimension=0, tiled=True)
            image = to_row_layout(piece, rows, cols)
        first = small_sum(product(stacked.T, image), "row")
        once = image - product(stacked, first)
        both = product(jnp.concatenate([stacked, once], axis=1).T, once)
        both = small_sum(both, "row")
        second, raw_gram = both[: (section + 1) * width], both[(section + 1) * width :]
        twice = once - product(stacked, second)
        gram = raw_gram - product(second.T, second)
        current, upper = finish_block(twice, gram)
        projection = projection.at[
            : (section + 1) * width, section * width : (section + 1) * width
        ].set(first + second)
        projection = projection.at[
            (section + 1) * width : (section + 2) * width, section * width : (section + 1) * width
        ].set(upper)
        first_pass = first_pass.at[
            : (section + 1) * width, section * width : (section + 1) * width
        ].set(first)
        blocks.append(current)
    basis = jnp.concatenate(blocks, axis=1) * jnp.float32(N**0.5)
    return (basis, projection, first_pass)


def solution(mesh):
    rows, cols = mesh.shape["row"], mesh.shape["col"]
    return jax.shard_map(
        lambda covariance, seed_index: solve(rows, cols, covariance, seed_index),
        mesh=mesh,
        in_specs=(P("row", "col"), P()),
        out_specs=(P("row", None), P(), P()),
        check_vma=False,
    )
```

time: 877 us -> 481 us (0.55)
  waiting for transfers between devices: 581 us -> 221 us
  matrix products: 137 us -> 73.5 us
  blocking collectives: 0 us -> 56.8 us
  local copies, waits for them, and re-layouts: 59.9 us -> 28.7 us
    psum x8 -> x2, waiting for transfers between devices: 406 us -> 124 us  [the longest x1 69 us: solve(): image = lax.psum(product(covariance, vector), 'col')]
    all_gather x2, waiting for transfers between devices: 175 us -> 70 us  [to_row_layout(): return lax.all_gather(moved, 'col', axis=0, tiled=True)]
    dot_general x15 -> x13, matrix products: 125 us -> 67.3 us  [product(): jnp.dot(left, right, precision=lax.Precision.HIGH, preferred_element_type...]
    all_gather x0 -> x5, blocking collectives: none -> 56.8 us  [small_sum(): return jnp.sum(lax.all_gather(value, axis, axis=0), axis=0)]
    unnamed x30 -> x25, local copies, waits for them, and re-layouts: 39.2 us -> 8.25 us
    reduce_scatter x0 -> x1, waiting for transfers between devices: none -> 26.5 us  [solve(): lax.psum_scatter(partial_value, 'row', scatter_dimension=0, tiled=True)]
  transfers between devices with their start and end apart: 10 -> 7, of which waited for: 10 -> 5; matrix products, arithmetic and copies ran while one was open for 0% -> 0% of each run, Pallas kernels for 0% -> 0%
where the time goes in v1:
time: 481 us; the launch traced here: 473 us
  waiting for transfers between devices  221 us (46%)
  other arithmetic  76.3 us (16%)
  matrix products  73.5 us (15%)
  blocking collectives  56.8 us (12%)
  local copies, waits for them, and re-layouts  28.7 us (6%)
  between operations  14.4 us (3%)
    all_gather x2, waiting for transfers between devices, to_row_layout(): return lax.all_gather(moved, 'col', axis=0, tiled=True)  70 us
    psum x1, waiting for transfers between devices, solve(): image = lax.psum(product(covariance, vector), 'col')  69 us
    dot_general x13, matrix products, product(): jnp.dot(left, right, precision=lax.Precision.HIGH, preferred_element_type...  67.3 us
    all_gather x5, blocking collectives, small_sum(): return jnp.sum(lax.all_gather(value, axis, axis=0), axis=0)  56.8 us
    psum x1, waiting for transfers between devices, solve(): start = lax.psum(jnp.where(inside[:, None], picked, 0.0), 'row').T  55.3 us
    another operation x9, other arithmetic, finish_block(): lower = jnp.linalg.cholesky(gram)  37.2 us
    another operation x4, other arithmetic, finish_block(): jax.scipy.linalg.solve_triangular(lower, block.T, lower=True)  30.1 us
    reduce_scatter x1, waiting for transfers between devices, solve(): lax.psum_scatter(partial_value, 'row', scatter_dimension=0, tiled=True)  26.5 us
  transfers between devices with their start and end apart: 7, of which 5 were waited for; matrix products, arithmetic and copies ran while one was open for 0% of the time, Pallas kernels for 0%

profile of v1, /device:TPU:0, one launch (start us, length us, event | category | flops | bytes accessed | tf_op | source)
XLA Modules:
  0.0 473.1 jit_solution(1931504965210466814)
XLA Ops:
  7.9 12.0 %gather_fusion = f32[128,2048]{1,0:T(8,128)S(1)} fusion(f32[4096,2048]{1,0:T(8,128)} %param.17, s32[1024]{0:T(1024)S(1)} %pad_clamp_fusion), kind=kCustom, calls=%fused_computation | custom fusion | bytes 2097664 | tf_op jit(solution)/shard_map/jit(_take)/gather | solution.py:37
  21.1 55.3 %all-reduce.5.cloned.1.call-done = f32[128,2048]{1,0:T(8,128)} async-done(((f32[128,2048]{1,0:T(8,128)}), f32[128,2048]{1,0:T(8,128)}) %all-reduce.5.cloned.1.call-update) | async-done | bytes 1048592 | tf_op jit(solution)/shard_map/psum | solution.py:38
  76.4 2.2 fusion.30
  78.7 14.8 %all-gather = f32[1024,128]{1,0:T(8,128)S(1)} all-gather(f32[128,128]{1,0:T(8,128)S(1)} %fusion.30), channel_id=2, replica_groups=mesh['row'=4,'col'=8] {'col'}, dimensions={0}, use_global_device_ids=true | all-gather | bytes 589824 | tf_op jit(solution)/shard_map/all_gather | solution.py:15
  93.6 11.7 %cholesky.59 = f32[128,128]{1,0:T(8,128)S(1)} custom-call(f32[128,128]{1,0:T(8,128)S(1)} %fusion.19), custom_call_target="Cholesky" | custom-call | tf_op jit(solution)/shard_map/jit(cholesky)/cholesky | solution.py:19
  106.6 9.8 %custom-call.9 = f32[1,128,128]{1,2,0:T(8,128)S(1)} custom-call(f32[1,128,128]{2,1,0:T(8,128)S(1)} %fusion.11), custom_call_target="InvertDiagBlocksLowerTriangular" | custom-call | tf_op jit(solution)/shard_map/jit(_solve_triangular)/triangular_solve | solution.py:20
  117.5 24.0 %convolution_bitcast_fusion.1 = f32[4096,128]{0,1:T(8,128)} fusion(f32[128,2048]{1,0:T(8,128)S(1)} %fusion.17, f32[4096,2048]{1,0:T(8,128)} %param.17), kind=kOutput, calls=%fused_computation.15 | convolution fusion | flops 6442450944 | bytes 36700160 | tf_op jit(solution)/shard_map/dot_general | solution.py:11
  143.1 69.0 %all-reduce.7.cloned.1.call-done = f32[4096,128]{0,1:T(8,128)} async-done(((f32[4096,128]{0,1:T(8,128)}), f32[4096,128]{0,1:T(8,128)}) %all-reduce.7.cloned.1.call-update) | async-done | bytes 2097168 | tf_op jit(solution)/shard_map/psum | solution.py:49
  212.1 31.0 %all-gather.8.cloned.1.call-done = f32[4096,128]{0,1:T(8,128)} async-done(((f32[512,128]{0,1:T(8,128)}), f32[4096,128]{0,1:T(8,128)}) %all-gather.8.cloned.1.call-update) | async-done | bytes 2097168 | tf_op jit(solution)/shard_map/all_gather | solution.py:27
  243.1 3.4 fusion.31
  246.5 8.9 %all-gather.1 = f32[512,128]{1,0:T(8,128)S(1)} all-gather(f32[128,128]{1,0:T(8,128)S(1)} %fusion.31), channel_id=3, replica_groups=mesh['row'=4,'col'=8] {'row'}, dimensions={0}, use_global_device_ids=true | all-gather | bytes 327680 | tf_op jit(solution)/shard_map/all_gather | solution.py:15
  255.4 2.7 convolution_subtract_fusion.3
  260.1 11.0 %all-gather.2 = f32[1024,128]{1,0:T(8,128)S(1)} all-gather(f32[256,128]{1,0:T(8,128)S(1)} %fusion.5), channel_id=4, replica_groups=mesh['row'=4,'col'=8] {'row'}, dimensions={0}, use_global_device_ids=true | all-gather | bytes 655360 | tf_op jit(solution)/shard_map/all_gather | solution.py:15
  271.6 11.7 %cholesky.70 = f32[128,128]{1,0:T(8,128)S(1)} custom-call(f32[128,128]{1,0:T(8,128)S(1)} %fusion.16), custom_call_target="Cholesky" | custom-call | tf_op jit(solution)/shard_map/jit(cholesky)/cholesky | solution.py:19
  284.6 9.8 %custom-call.11 = f32[1,128,128]{1,2,0:T(8,128)S(1)} custom-call(f32[1,128,128]{2,1,0:T(8,128)S(1)} %get-tuple-element.92), custom_call_target="InvertDiagBlocksLowerTriangular" | custom-call | tf_op jit(solution)/shard_map/jit(_solve_triangular)/triangular_solve | solution.py:20
  294.4 2.7 fusion.4
  297.1 3.3 fusion.14
  300.4 15.8 %convolution_bitcast_fusion.2 = f32[2048,128]{0,1:T(8,128)} fusion(f32[128,4096]{1,0:T(8,128)} %fusion.14, f32[4096,2048]{1,0:T(8,128)} %param.17), kind=kOutput, calls=%fused_computation.19 | convolution fusion | flops 6442450944 | bytes 36700160 | tf_op jit(solution)/shard_map/dot_general | solution.py:11
  316.2 26.5 %reduce-scatter.2.cloned.1.call-done = f32[512,128]{0,1:T(8,128)} async-done(((f32[2048,128]{0,1:T(8,128)}), f32[512,128]{0,1:T(8,128)}) %reduce-scatter.2.cloned.1.call-update) | async-done | bytes 262160 | tf_op jit(solution)/shard_map/reduce_scatter | solution.py:52
  347.5 39.0 %all-gather.10.cloned.1.call-done = f32[4096,128]{0,1:T(8,128)} async-done(((f32[512,128]{0,1:T(8,128)}), f32[4096,128]{0,1:T(8,128)}) %all-gather.10.cloned.1.call-update) | async-done | bytes 2097168 | tf_op jit(solution)/shard_map/all_gather | solution.py:27
  386.5 4.0 fusion.7
  390.5 10.0 %all-gather.3 = f32[1024,128]{1,0:T(8,128)S(1)} all-gather(f32[256,128]{1,0:T(8,128)S(1)} %fusion.7), channel_id=5, replica_groups=mesh['row'=4,'col'=8] {'row'}, dimensions={0}, use_global_device_ids=true | all-gather | bytes 655360 | tf_op jit(solution)/shard_map/all_gather | solution.py:15
  400.6 3.7 convolution_subtract_fusion.1
  404.3 2.7 fusion
  407.0 12.1 %all-gather.4 = f32[1536,128]{1,0:T(8,128)S(1)} all-gather(f32[384,128]{1,0:T(8,128)S(1)} %fusion), channel_id=6, replica_groups=mesh['row'=4,'col'=8] {'row'}, dimensions={0}, use_global_device_ids=true | all-gather | bytes 983040 | tf_op jit(solution)/shard_map/all_gather | solution.py:15
  419.7 11.7 %cholesky.81 = f32[128,128]{1,0:T(8,128)S(1)} custom-call(f32[128,128]{1,0:T(8,128)S(1)} %fusion.13), custom_call_target="Cholesky" | custom-call | tf_op jit(solution)/shard_map/jit(cholesky)/cholesky | solution.py:19
  432.7 9.8 %custom-call.12 = f32[1,128,128]{1,2,0:T(8,128)S(1)} custom-call(f32[1,128,128]{2,1,0:T(8,128)S(1)} %get-tuple-element.90), custom_call_target="InvertDiagBlocksLowerTriangular" | custom-call | tf_op jit(solution)/shard_map/jit(_solve_triangular)/triangular_solve | solution.py:20
  442.5 3.6 fusion.3
  448.1 3.0 maximum_multiply_fusion
  451.1 6.6 %copy.22 = f32[4096,384]{1,0:T(8,128)} copy(f32[4096,384]{0,1:T(8,128)} %maximum_multiply_fusion) | data formatting | bytes 12582912
  459.7 2.8 scatter.24
  462.6 3.7 scatter.29
  (79 shorter events, 20.3 us)
Async XLA Ops:
  7.2 69.3 %all-reduce.5.cloned.1.call-start = ((), (), s32[]{:S(2)}) async-start(), calls=%async_computation.1 | async-start | bytes 2097152 | tf_op jit(solution)/shard_map/psum | solution.py:38
  21.1 191.0 %all-reduce.7.cloned.1.call-start = ((), (), s32[]{:S(2)}) async-start(), calls=%async_computation.3 | async-start | bytes 4194304 | tf_op jit(solution)/shard_map/psum | solution.py:49
  76.4 40.0 %copy-start.4 = (f32[128,2048]{1,0:T(8,128)S(1)}, f32[128,2048]{1,0:T(8,128)}, u32[]{:S(2)}) copy-start(f32[128,2048]{1,0:T(8,128)} %all-reduce.5.cloned.1.call-done) | copy-start | bytes 3145732
  141.6 101.5 %all-gather.8.cloned.1.call-start = ((), (), s32[]{:S(2)}) async-start(), calls=%async_computation.2 | async-start | bytes 2359296 | tf_op jit(solution)/shard_map/all_gather | solution.py:27
  141.6 0.7 collective-permute-start
  142.3 0.7 copy-start.10
  143.1 199.7 %reduce-scatter.2.cloned.1.call-start = ((), (), s32[]{:S(2)}) async-start(), calls=%async_computation.4 | async-start | bytes 1310720 | tf_op jit(solution)/shard_map/reduce_scatter | solution.py:52
  243.1 12.4 %copy-start = (f32[4096,128]{0,1:T(8,128)S(1)}, f32[4096,128]{0,1:T(8,128)}, u32[]{:S(2)}) copy-start(f32[4096,128]{0,1:T(8,128)} %all-gather.8.cloned.1.call-done) | copy-start | bytes 6291460
  258.1 1.9 copy-start.3
  316.2 70.3 %all-gather.10.cloned.1.call-start = ((), (), s32[]{:S(2)}) async-start(), calls=%async_computation.5 | async-start | bytes 2359296 | tf_op jit(solution)/shard_map/all_gather | solution.py:27
  342.7 1.8 collective-permute-start.1
  344.5 0.7 copy-start.9
  347.5 39.0 %copy-start.6 = (f32[384,256]{1,0:T(8,128)}, f32[384,256]{1,0:T(8,128)S(1)}, u32[]{:S(2)}) copy-start(f32[384,256]{1,0:T(8,128)S(1)} %constant_dynamic-update-slice_fusion.1) | copy-start | bytes 1179652
  400.6 3.7 copy-start.1
  404.3 2.7 copy-start.5
  446.1 2.0 copy-start.2
  451.1 6.6 %copy-start.7 = (f32[384,256]{1,0:T(8,128)S(1)}, f32[384,256]{1,0:T(8,128)}, u32[]{:S(2)}) copy-start(f32[384,256]{1,0:T(8,128)} %copy-done.6) | copy-start | bytes 1179652
  462.6 3.8 copy-start.8
Sparse Core Ops, SparseCore 0:
  21.2 55.1 all-reduce.4
  141.7 70.3 all-reduce.6
  214.3 28.7 all-gather.7
  316.3 26.4 reduce-scatter.1
  345.4 41.0 all-gather.9
